TPU v7x, 32 devices: a whole 2x2x4 slice. The times are simulated.
32 devices in a mesh: row: 4 (over y, x), col: 8 (over z, core).
Axes of the slice: x: 2, y: 2, z: 4, core: 2. Of those that a mesh axis runs over, the one named last changes fastest.
Arguments:
- gradient: bfloat16 [2304, 18432], P('row', 'col'), may hold values from -6 to 6
- left_basis: bfloat16 [2304, 2304], P('row'), may hold values from -0.125 to 0.125
- right_basis: bfloat16 [18432, 18432], P('col', 'row'), may hold values from -0.046875 to 0.046875
- first_moment: float32 [2304, 18432], P('col', 'row'), may hold values from -3 to 3
- second_moment: float32 [2304, 18432], P('col', 'row'), may hold values from 0.25 to 4
Outputs:
- update: bfloat16 [2304, 18432], P('row', 'col')
- first_new: float32 [2304, 18432], P('col', 'row')
- second_new: float32 [2304, 18432], P('col', 'row')
All inputs are finite; a program needn't handle non-finite values.
Results may differ from a plain program's by a relative error of at most 0.018.
Values may be sent and summed in bfloat16 or wider, within the bound.
A program may use at most 128 MiB of HBM per device.

v0:
```python
import jax
import jax.numpy as jnp
from jax import lax
from jax.sharding import PartitionSpec as P

beta_one = 0.9
beta_two = 0.95
epsilon = 1e-08
correct_one = 1.0 - 0.9**10
correct_two = 1.0 - 0.95**10


def per_device(gradient, left_basis, right_basis, first_moment, second_moment):
    partial_value = lax.dot_general(
        left_basis, gradient, (((0,), (0,)), ((), ())), preferred_element_type=jnp.float32
    )
    rotated_left = lax.psum(partial_value.astype(jnp.bfloat16), "row")
    rotated = lax.psum_scatter(
        jnp.dot(rotated_left, right_basis, preferred_element_type=jnp.float32).astype(jnp.bfloat16),
        "col",
        scatter_dimension=0,
        tiled=True,
    )
    rotated_wide = rotated.astype(jnp.float32)
    first_new = beta_one * first_moment + (1.0 - beta_one) * rotated_wide
    second_new = beta_two * second_moment + (1.0 - beta_two) * rotated_wide * rotated_wide
    step_rot = (first_new / correct_one / (jnp.sqrt(second_new / correct_two) + epsilon)).astype(
        jnp.bfloat16
    )
    back_part = lax.dot_general(
        lax.all_gather(step_rot, "col", axis=0, tiled=True),
        right_basis,
        (((1,), (1,)), ((), ())),
        preferred_element_type=jnp.float32,
    )
    back_own = lax.psum_scatter(
        back_part.astype(jnp.bfloat16), "row", scatter_dimension=0, tiled=True
    )
    back_rot = lax.all_gather(back_own, "row", axis=0, tiled=True)
    update = jnp.dot(left_basis, back_rot, preferred_element_type=jnp.float32).astype(jnp.bfloat16)
    return (update, first_new, second_new)


def solution(mesh):
    in_specs = (P("row", "col"), P("row", None), P("col", "row"), P("col", "row"), P("col", "row"))
    out_specs = (P("row", "col"), P("col", "row"), P("col", "row"))
    return jax.shard_map(
        per_device, mesh=mesh, in_specs=in_specs, out_specs=out_specs, check_vma=False
    )
```

profile of v0, /device:TPU:0, one launch (start us, length us, event | category | flops | bytes accessed | tf_op | source)
XLA Modules:
  0.0 982.5 jit_solution(14175952818253568337)
XLA Ops:
  7.2 0.0 copy-start
  7.2 0.0 all-reduce.2.cloned.1.call-start
  7.2 1.7 copy-done
  8.9 12.5 %convolution_convert_fusion.2 = bf16[2304,2304]{1,0:T(8,128)(2,1)} fusion(bf16[576,2304]{1,0:T(8,128)(2,1)S(1)} %copy-done, bf16[576,2304]{1,0:T(8,128)(2,1)} %param.5), kind=kOutput, calls=%fused_computation.2 | convolution fusion | flops 6120603648 | bytes 15925248 | tf_op jit(solution)/shard_map/dot_general | solution.py:14
  21.4 0.0 all-reduce.2.cloned.1.call-update
  21.4 0.0 reduce-scatter.3.cloned.1.call-start
  21.5 210.5 %all-reduce.2.cloned.1.call-done = bf16[2304,2304]{1,0:T(8,128)(2,1)} async-done(((bf16[2304,2304]{1,0:T(8,128)(2,1)}), bf16[2304,2304]{1,0:T(8,128)(2,1)}) %all-reduce.2.cloned.1.call-update) | async-done | bytes 10616848 | tf_op jit(solution)/shard_map/psum | solution.py:17
  232.0 57.8 %convolution_convert_fusion = bf16[2304,4608]{1,0:T(8,128)(2,1)} fusion(bf16[2304,2304]{1,0:T(8,128)(2,1)} %all-reduce.2.cloned.1.call-done, bf16[2304,4608]{1,0:T(8,128)(2,1)} %param.7), kind=kOutput, calls=%fused_computation | convolution fusion | flops 48932978688 | bytes 53084160 | tf_op jit(solution)/shard_map/dot_general | solution.py:19
  289.7 0.0 reduce-scatter.3.cloned.1.call-update
  289.8 0.2 all-gather.3.cloned.1.call-start
  290.0 210.0 %reduce-scatter.3.cloned.1.call-done = bf16[288,4608]{1,0:T(8,128)(2,1)} async-done(((bf16[2304,4608]{1,0:T(8,128)(2,1)}), bf16[288,4608]{1,0:T(8,128)(2,1)}) %reduce-scatter.3.cloned.1.call-update) | async-done | bytes 2654224 | tf_op jit(solution)/shard_map/reduce_scatter | solution.py:18
  500.0 9.4 divide_convert_fusion
  509.4 0.0 all-gather.3.cloned.1.call-update
  509.4 0.0 reduce-scatter.5.cloned.1.call-start
  509.5 186.2 %all-gather.3.cloned.1.call-done = bf16[2304,4608]{1,0:T(8,128)(2,1)} async-done(((bf16[288,4608]{1,0:T(8,128)(2,1)}), bf16[2304,4608]{1,0:T(8,128)(2,1)}) %all-gather.3.cloned.1.call-update) | async-done | bytes 21233680 | tf_op jit(solution)/shard_map/all_gather | solution.py:31
  695.7 58.1 %convolution_convert_fusion.1 = bf16[2304,2304]{1,0:T(8,128)(2,1)} fusion(bf16[2304,4608]{1,0:T(8,128)(2,1)} %all-gather.3.cloned.1.call-done, bf16[2304,4608]{1,0:T(8,128)(2,1)} %param.7), kind=kOutput, calls=%fused_computation.1 | convolution fusion | flops 48927670272 | bytes 53084160 | tf_op jit(solution)/shard_map/dot_general | solution.py:30
  753.7 0.0 reduce-scatter.5.cloned.1.call-update
  753.8 0.0 all-gather.5.cloned.1.call-start
  753.8 102.8 %reduce-scatter.5.cloned.1.call-done = bf16[576,2304]{1,0:T(8,128)(2,1)} async-done(((bf16[2304,2304]{1,0:T(8,128)(2,1)}), bf16[576,2304]{1,0:T(8,128)(2,1)}) %reduce-scatter.5.cloned.1.call-update) | async-done | bytes 2654224 | tf_op jit(solution)/shard_map/reduce_scatter | solution.py:36
  856.6 0.0 all-gather.5.cloned.1.call-update
  856.7 107.7 %all-gather.5.cloned.1.call-done = bf16[2304,2304]{1,0:T(8,128)(2,1)} async-done(((bf16[576,2304]{1,0:T(8,128)(2,1)}), bf16[2304,2304]{1,0:T(8,128)(2,1)}) %all-gather.5.cloned.1.call-update) | async-done | bytes 10616848 | tf_op jit(solution)/shard_map/all_gather | solution.py:39
  964.4 11.6 %fusion.2 = bf16[576,2304]{1,0:T(8,128)(2,1)} fusion(bf16[576,2304]{1,0:T(8,128)(2,1)S(1)} %copy-done, bf16[2304,2304]{1,0:T(8,128)(2,1)} %all-gather.5.cloned.1.call-done), kind=kOutput, calls=%fused_computation.9 | convolution fusion | flops 6116622336 | bytes 15925248 | tf_op jit(solution)/shard_map/dot_general | solution.py:40
Async XLA Ops:
  7.2 1.8 copy-start
  7.2 224.8 %all-reduce.2.cloned.1.call-start = ((), (), s32[]{:S(2)}) async-start(), calls=%async_computation.2 | async-start | bytes 21233664 | tf_op jit(solution)/shard_map/psum | solution.py:17
  21.4 478.6 %reduce-scatter.3.cloned.1.call-start = ((), (), s32[]{:S(2)}) async-start(), calls=%async_computation.3 | async-start | bytes 23887872 | tf_op jit(solution)/shard_map/reduce_scatter | solution.py:18
  289.8 405.9 %all-gather.3.cloned.1.call-start = ((), (), s32[]{:S(2)}) async-start(), calls=%async_computation.4 | async-start | bytes 23887872 | tf_op jit(solution)/shard_map/all_gather | solution.py:31
  509.4 347.2 %reduce-scatter.5.cloned.1.call-start = ((), (), s32[]{:S(2)}) async-start(), calls=%async_computation.5 | async-start | bytes 13271040 | tf_op jit(solution)/shard_map/reduce_scatter | solution.py:36
  753.8 210.6 %all-gather.5.cloned.1.call-start = ((), (), s32[]{:S(2)}) async-start(), calls=%async_computation.6 | async-start | bytes 13271040 | tf_op jit(solution)/shard_map/all_gather | solution.py:39
Sparse Core Ops, SparseCore 0:
  21.6 210.3 all-reduce.1
  289.9 210.0 reduce-scatter.2
  509.6 186.0 all-gather.2
  753.9 102.7 reduce-scatter.4
  858.3 106.0 all-gather.4
where the time goes:
time: 983 us
  waiting for transfers between devices  817 us (83%)
  matrix products  140 us (14%)
  between operations  13.8 us (1%)
    psum x1, waiting for transfers between devices, per_device(): rotated_left = lax.psum(partial_value.astype(jnp.bfloat16), 'row')  210 us
    reduce_scatter x1, waiting for transfers between devices, per_device(): lax.psum_scatter(jnp.dot(rotated_left, right_basis, preferred_element_typ...  210 us
    all_gather x1, waiting for transfers between devices, per_device(): lax.all_gather(step_rot, 'col', axis=0, tiled=True)  186 us
    all_gather x1, waiting for transfers between devices, per_device(): back_rot = lax.all_gather(back_own, 'row', axis=0, tiled=True)  108 us
    reduce_scatter x1, waiting for transfers between devices, per_device(): lax.psum_scatter(back_part.astype(jnp.bfloat16), 'row', scatter_dimension...  103 us
    dot_general x1, matrix products, per_device(): lax.dot_general(lax.all_gather(step_rot, 'col', axis=0, tiled=True), righ...  58.1 us
    dot_general x1, matrix products, per_device(): jnp.dot(rotated_left, right_basis, preferred_element_type=jnp.float32)  57.8 us
  transfers between devices with their start and end apart: 5, of which 5 were waited for; matrix products, arithmetic and copies ran while one was open for 0% of the time, Pallas kernels for 0%

commit v1 on v0

--- a/solution.py
+++ b/solution.py
@@ -14,7 +14,7 @@
     partial_value = lax.dot_general(
         left_basis, gradient, (((0,), (0,)), ((), ())), preferred_element_type=jnp.float32
     )
-    rotated_left = lax.psum(partial_value.astype(jnp.bfloat16), "row")
+    rotated_left = jnp.sum(lax.all_gather(partial_value.astype(jnp.bfloat16), "row"), axis=0)
     rotated = lax.psum_scatter(
         jnp.dot(rotated_left, right_basis, preferred_element_type=jnp.float32).astype(jnp.bfloat16),
         "col",

time: 983 us -> 1180 us (1.20)
  waiting for transfers between devices: 817 us -> 981 us
  other arithmetic: 9.39 us -> 44.1 us
    all_gather x0 -> x1, waiting for transfers between devices: none -> 374 us  [per_device(): lax.all_gather(partial_value.astype(jnp.bfloat16), 'row')]
    psum x1 -> x0, waiting for transfers between devices: 210 us -> none  [per_device(): rotated_left = lax.psum(partial_value.astype(jnp.bfloat16), 'row')]
    reduce_sum x0 -> x1, other arithmetic: none -> 34.7 us  [per_device(): jnp.sum(lax.all_gather(partial_value.astype(jnp.bfloat16), 'row'), axis=0)]
where the time goes in v1:
time: 1180 us
  waiting for transfers between devices  981 us (83%)
  matrix products  140 us (12%)
  other arithmetic  44.1 us (4%)
  between operations  13.8 us (1%)
    all_gather x1, waiting for transfers between devices, per_device(): lax.all_gather(partial_value.astype(jnp.bfloat16), 'row')  374 us
    reduce_scatter x1, waiting for transfers between devices, per_device(): lax.psum_scatter(jnp.dot(rotated_left, right_basis, preferred_element_typ...  210 us
    all_gather x1, waiting for transfers between devices, per_device(): lax.all_gather(step_rot, 'col', axis=0, tiled=True)  186 us
    all_gather x1, waiting for transfers between devices, per_device(): back_rot = lax.all_gather(back_own, 'row', axis=0, tiled=True)  108 us
    reduce_scatter x1, waiting for transfers between devices, per_device(): lax.psum_scatter(back_part.astype(jnp.bfloat16), 'row', scatter_dimension...  103 us
    dot_general x1, matrix products, per_device(): lax.dot_general(lax.all_gather(step_rot, 'col', axis=0, tiled=True), righ...  58.1 us
    dot_general x1, matrix products, per_device(): jnp.dot(rotated_left, right_basis, preferred_element_type=jnp.float32)  57.8 us
    reduce_sum x1, other arithmetic, per_device(): jnp.sum(lax.all_gather(partial_value.astype(jnp.bfloat16), 'row'), axis=0)  34.7 us
  transfers between devices with their start and end apart: 5, of which 5 were waited for; matrix products, arithmetic and copies ran while one was open for 0% of the time, Pallas kernels for 0%

profile of v1, /device:TPU:0, one launch (start us, length us, event | category | flops | bytes accessed | tf_op | source)
XLA Modules:
  0.0 1181.1 jit_solution(2363118378023920362)
XLA Ops:
  7.2 0.0 copy-start
  7.2 0.0 all-gather.9.cloned.1.call-start
  7.2 1.7 copy-done
  8.9 12.4 %convolution_convert_fusion.2 = bf16[2304,2304]{1,0:T(8,128)(2,1)} fusion(bf16[576,2304]{1,0:T(8,128)(2,1)S(1)} %copy-done, bf16[576,2304]{1,0:T(8,128)(2,1)} %param.5), kind=kOutput, calls=%fused_computation.2 | convolution fusion | flops 6120603648 | bytes 15925248 | tf_op jit(solution)/shard_map/dot_general | solution.py:14
  21.3 0.0 all-gather.9.cloned.1.call-update
  21.4 0.2 reduce-scatter.3.cloned.1.call-start
  21.6 374.3 %all-gather.9.cloned.1.call-done = bf16[9216,2304]{1,0:T(8,128)(2,1)} async-done(((bf16[2304,2304]{1,0:T(8,128)(2,1)}), bf16[9216,2304]{1,0:T(8,128)(2,1)}) %all-gather.9.cloned.1.call-update) | async-done | bytes 42467344 | tf_op jit(solution)/shard_map/all_gather | solution.py:17
  395.9 34.7 %reduce_sum.12 = bf16[2304,2304]{1,0:T(8,128)(2,1)} reduce(bf16[4,2304,2304]{2,1,0:T(8,128)(2,1)} %bitcast.11, bf16[]{:T(256)} %constant.4.clone.1), dimensions={0}, to_apply=%region_0.0 | reduce | flops 15925248 | bytes 53084160 | tf_op jit(solution)/shard_map/reduce_sum | solution.py:17
  430.6 57.8 %convolution_convert_fusion = bf16[2304,4608]{1,0:T(8,128)(2,1)} fusion(bf16[2304,2304]{1,0:T(8,128)(2,1)} %reduce_sum.12, bf16[2304,4608]{1,0:T(8,128)(2,1)} %param.7), kind=kOutput, calls=%fused_computation | convolution fusion | flops 48932978688 | bytes 53084160 | tf_op jit(solution)/shard_map/dot_general | solution.py:19
  488.4 0.0 reduce-scatter.3.cloned.1.call-update
  488.4 0.3 all-gather.5.cloned.1.call-start
  488.7 210.0 %reduce-scatter.3.cloned.1.call-done = bf16[288,4608]{1,0:T(8,128)(2,1)} async-done(((bf16[2304,4608]{1,0:T(8,128)(2,1)}), bf16[288,4608]{1,0:T(8,128)(2,1)}) %reduce-scatter.3.cloned.1.call-update) | async-done | bytes 2654224 | tf_op jit(solution)/shard_map/reduce_scatter | solution.py:18
  698.7 9.4 divide_convert_fusion
  708.1 0.0 all-gather.5.cloned.1.call-update
  708.1 0.0 reduce-scatter.5.cloned.1.call-start
  708.1 186.2 %all-gather.5.cloned.1.call-done = bf16[2304,4608]{1,0:T(8,128)(2,1)} async-done(((bf16[288,4608]{1,0:T(8,128)(2,1)}), bf16[2304,4608]{1,0:T(8,128)(2,1)}) %all-gather.5.cloned.1.call-update) | async-done | bytes 21233680 | tf_op jit(solution)/shard_map/all_gather | solution.py:31
  894.3 58.1 %convolution_convert_fusion.1 = bf16[2304,2304]{1,0:T(8,128)(2,1)} fusion(bf16[2304,4608]{1,0:T(8,128)(2,1)} %all-gather.5.cloned.1.call-done, bf16[2304,4608]{1,0:T(8,128)(2,1)} %param.7), kind=kOutput, calls=%fused_computation.1 | convolution fusion | flops 48927670272 | bytes 53084160 | tf_op jit(solution)/shard_map/dot_general | solution.py:30
  952.4 0.0 reduce-scatter.5.cloned.1.call-update
  952.4 0.0 all-gather.7.cloned.1.call-start
  952.5 102.8 %reduce-scatter.5.cloned.1.call-done = bf16[576,2304]{1,0:T(8,128)(2,1)} async-done(((bf16[2304,2304]{1,0:T(8,128)(2,1)}), bf16[576,2304]{1,0:T(8,128)(2,1)}) %reduce-scatter.5.cloned.1.call-update) | async-done | bytes 2654224 | tf_op jit(solution)/shard_map/reduce_scatter | solution.py:36
  1055.3 0.0 all-gather.7.cloned.1.call-update
  1055.3 107.7 %all-gather.7.cloned.1.call-done = bf16[2304,2304]{1,0:T(8,128)(2,1)} async-done(((bf16[576,2304]{1,0:T(8,128)(2,1)}), bf16[2304,2304]{1,0:T(8,128)(2,1)}) %all-gather.7.cloned.1.call-update) | async-done | bytes 10616848 | tf_op jit(solution)/shard_map/all_gather | solution.py:39
  1163.0 11.6 fusion.2
Async XLA Ops:
  7.2 1.8 copy-start
  7.2 388.8 %all-gather.9.cloned.1.call-start = ((), (), s32[]{:S(2)}) async-start(), calls=%async_computation.6 | async-start | bytes 53084160 | tf_op jit(solution)/shard_map/all_gather | solution.py:17
  21.4 677.3 %reduce-scatter.3.cloned.1.call-start = ((), (), s32[]{:S(2)}) async-start(), calls=%async_computation.2 | async-start | bytes 23887872 | tf_op jit(solution)/shard_map/reduce_scatter | solution.py:18
  488.4 405.9 %all-gather.5.cloned.1.call-start = ((), (), s32[]{:S(2)}) async-start(), calls=%async_computation.3 | async-start | bytes 23887872 | tf_op jit(solution)/shard_map/all_gather | solution.py:31
  708.1 347.2 %reduce-scatter.5.cloned.1.call-start = ((), (), s32[]{:S(2)}) async-start(), calls=%async_computation.4 | async-start | bytes 13271040 | tf_op jit(solution)/shard_map/reduce_scatter | solution.py:36
  952.4 210.6 %all-gather.7.cloned.1.call-start = ((), (), s32[]{:S(2)}) async-start(), calls=%async_computation.5 | async-start | bytes 13271040 | tf_op jit(solution)/shard_map/all_gather | solution.py:39
Sparse Core Ops, SparseCore 0:
  21.5 374.3 all-gather.8
  488.5 210.0 reduce-scatter.2
  708.2 186.0 all-gather.4
  952.5 102.7 reduce-scatter.4
  1057.0 106.0 all-gather.6
